TPU v7x, 32 devices: a whole 2x2x4 slice. The times are simulated.
32 devices in a mesh: groups: 2 (over x), seq: 16 (over z, y, core).
Axes of the slice: x: 2, y: 2, z: 4, core: 2. Of those that a mesh axis runs over, the one named last changes fastest.
Arguments:
- queries: bfloat16 [4, 128, 8192], P(None, ('groups', 'seq')), parts along dimension 1, may hold values from -16 to 16
- new_keys: bfloat16 [4, 128, 1024], P(None, ('groups', 'seq')), parts along dimension 1, may hold values from -6 to 6
- new_values: bfloat16 [4, 128, 1024], P(None, ('groups', 'seq')), parts along dimension 1, may hold values from -6 to 6
- pool_keys: bfloat16 [2048, 16, 1024], P(('groups', 'seq')), parts along dimension 0, may hold values from -6 to 6
- pool_values: bfloat16 [2048, 16, 1024], P(('groups', 'seq')), parts along dimension 0, may hold values from -6 to 6
- page_table: int32 [128, 16], P(('groups', 'seq')), parts along dimension 0, may hold values from 0 to 63, as said below
- cached_len: int32 [128], P(('groups', 'seq')), parts along dimension 0, may hold values from 1 to 256
- turn_keys: bfloat16 [4, 32, 16, 1024], P(None, ('groups', 'seq')), parts along dimension 1, may hold values from -6 to 6
- turn_values: bfloat16 [4, 32, 16, 1024], P(None, ('groups', 'seq')), parts along dimension 1, may hold values from -6 to 6
- turn_lengths: int32 [32], P('groups'), parts along dimension 0, may hold values from 1 to 80, 768 in all
- turn_slot: int32 [32], P('groups'), parts along dimension 0, may hold values from 0 to 63, as said below
Outputs:
- attended: bfloat16 [4, 128, 8192], P(None, ('groups', 'seq')), parts along dimension 1
- landed_keys: bfloat16 [32, 80, 1024], P(('groups', 'seq')), parts along dimension 0
- landed_values: bfloat16 [32, 80, 1024], P(('groups', 'seq')), parts along dimension 0
There are 2 independent parts, one for each index of `groups`. A program takes and returns all parts, laid end to end along the dimension named above; each array names one. Nothing has to cross between parts.
Inputs may be any that keep to these rules, and one draw needn't show every extreme that they name: `page_table`: the 4 rows of each device's slots together hold every number of 0 to 63 exactly once. `turn_lengths`: they sum to 768; the largest is exactly 80. `turn_slot`: each block of 4 slots holds the slot of exactly one turn.
All inputs are finite; a program needn't handle non-finite values.
Results may differ from a plain program's by a relative error of at most 0.0049.
Values may be sent and summed in bfloat16 or wider, within the bound.
A program may use at most 128 MiB of HBM per device.

v0:
```python
import math

import jax
import jax.numpy as jnp
from jax import lax
from jax.sharding import PartitionSpec as P

QH = 64
KVH = 8
HD = 128
MOSTT = 80


def per_device(
    queries,
    new_keys,
    new_values,
    pool_keys,
    pool_values,
    page_table,
    cached_len,
    turn_keys,
    turn_values,
    turn_lengths,
    turn_slot,
):
    chain_size = lax.axis_size("seq")
    own_index = lax.axis_index("seq")
    step_count, slots_here, query_width = queries.shape
    page_rows = pool_keys.shape[1]
    kv_width = pool_keys.shape[2]
    group_pages = turn_keys.shape[0]
    most_pages = -(-MOSTT // page_rows)
    page_counts = (turn_lengths + page_rows - 1) // page_rows
    page_starts = jnp.cumsum(page_counts) - page_counts
    owner_ids = turn_slot // slots_here
    owned = owner_ids == own_index
    my_length = jnp.sum(jnp.where(owned, turn_lengths, 0))
    my_slot = jnp.sum(jnp.where(owned, turn_slot % slots_here, 0))
    page_width = page_rows * kv_width
    slice_width = page_width // chain_size
    local_keys = turn_keys.reshape(group_pages, chain_size, slice_width)
    local_values = turn_values.reshape(group_pages, chain_size, slice_width)
    sliced_keys, sliced_values = (
        lax.all_to_all(local_keys, "seq", split_axis=1, concat_axis=1, tiled=True),
        lax.all_to_all(local_values, "seq", split_axis=1, concat_axis=1, tiled=True),
    )
    packed_keys = sliced_keys.reshape(group_pages * chain_size, slice_width)
    packed_values = sliced_values.reshape(group_pages * chain_size, slice_width)
    device_ids = jnp.arange(chain_size, dtype=jnp.int32)
    owner_match = owner_ids[None, :] == device_ids[:, None]
    owner_start = jnp.sum(jnp.where(owner_match, page_starts[None, :], 0), axis=1)
    owner_count = jnp.sum(jnp.where(owner_match, page_counts[None, :], 0), axis=1)
    wanted = owner_start[:, None] + jnp.arange(most_pages)[None, :]
    present = jnp.arange(most_pages)[None, :] < owner_count[:, None]
    picker = (jnp.arange(group_pages * chain_size)[None, None, :] == wanted[:, :, None]) & present[
        :, :, None
    ]
    picker = picker.astype(jnp.bfloat16).reshape(chain_size * most_pages, group_pages * chain_size)
    send_keys = jnp.dot(picker, packed_keys, preferred_element_type=jnp.float32).astype(
        jnp.bfloat16
    )
    send_values = jnp.dot(picker, packed_values, preferred_element_type=jnp.float32).astype(
        jnp.bfloat16
    )
    send_keys = send_keys.reshape(chain_size, most_pages, slice_width)
    send_values = send_values.reshape(chain_size, most_pages, slice_width)
    arrived_keys, arrived_values = (
        lax.all_to_all(send_keys, "seq", split_axis=0, concat_axis=2, tiled=True),
        lax.all_to_all(send_values, "seq", split_axis=0, concat_axis=2, tiled=True),
    )
    got_keys = arrived_keys.reshape(most_pages, page_width)
    got_values = arrived_values.reshape(most_pages, page_width)
    fresh_span = most_pages * page_rows
    keeping = (jnp.arange(fresh_span) < my_length)[:, None]
    token_keys = got_keys.reshape(fresh_span, kv_width)
    token_values = got_values.reshape(fresh_span, kv_width)
    landed_keys = jnp.where(keeping, token_keys, jnp.zeros_like(token_keys))
    landed_values = jnp.where(keeping, token_values, jnp.zeros_like(token_values))
    group_share = QH // KVH
    score_scale = 1.0 / math.sqrt(HD)
    query_heads = queries.reshape(step_count, slots_here, KVH, group_share, HD)
    pool_rows = page_table.reshape(-1)
    resident_keys = pool_keys[pool_rows].reshape(slots_here, -1, KVH, HD)
    resident_values = pool_values[pool_rows].reshape(slots_here, -1, KVH, HD)
    token_span = resident_keys.shape[1]
    score_res = (
        jnp.einsum(
            "srgeh,rcgh->srgec", query_heads, resident_keys, preferred_element_type=jnp.float32
        )
        * score_scale
    )
    keep_res = jnp.arange(token_span)[None, :] < cached_len[:, None]
    score_res = jnp.where(keep_res[None, :, None, None, :], score_res, -jnp.inf)
    decode_keys = new_keys.reshape(step_count, slots_here, KVH, HD)
    decode_values = new_values.reshape(step_count, slots_here, KVH, HD)
    score_new = (
        jnp.einsum(
            "srgeh,trgh->srget", query_heads, decode_keys, preferred_element_type=jnp.float32
        )
        * score_scale
    )
    causal_mask = jnp.arange(step_count)[None, :] <= jnp.arange(step_count)[:, None]
    score_new = jnp.where(causal_mask[:, None, None, None, :], score_new, -jnp.inf)
    largest = jnp.maximum(jnp.max(score_res, axis=-1), jnp.max(score_new, axis=-1))
    fresh_keys = landed_keys.reshape(fresh_span, KVH, HD)
    fresh_values = landed_values.reshape(fresh_span, KVH, HD)
    query_mine = lax.dynamic_index_in_dim(query_heads, my_slot, 1, keepdims=False)
    score_fresh = (
        jnp.einsum("sgeh,cgh->sgec", query_mine, fresh_keys, preferred_element_type=jnp.float32)
        * score_scale
    )
    keep_fresh = jnp.arange(fresh_span) < my_length
    score_fresh = jnp.where(keep_fresh, score_fresh, -jnp.inf)
    largest_mine = jnp.maximum(
        lax.dynamic_index_in_dim(largest, my_slot, 1, keepdims=False), jnp.max(score_fresh, axis=-1)
    )
    chosen = (jnp.arange(slots_here) == my_slot)[None, :, None, None]
    largest = jnp.where(chosen, largest_mine[:, None], largest)
    prob_res = jnp.exp(score_res - largest[..., None])
    prob_new = jnp.exp(score_new - largest[..., None])
    prob_fresh = jnp.exp(score_fresh - largest_mine[..., None])
    totals = jnp.sum(prob_res, axis=-1) + jnp.sum(prob_new, axis=-1)
    totals = totals + jnp.where(chosen, jnp.sum(prob_fresh, axis=-1)[:, None], 0.0)
    summed = jnp.einsum("srgec,rcgh->srgeh", prob_res, resident_values.astype(jnp.float32))
    summed = summed + jnp.einsum("srget,trgh->srgeh", prob_new, decode_values.astype(jnp.float32))
    summed_fresh = jnp.einsum("sgec,cgh->sgeh", prob_fresh, fresh_values.astype(jnp.float32))
    summed = summed + jnp.where(chosen[..., None], summed_fresh[:, None], 0.0)
    attended = (
        (summed / totals[..., None])
        .reshape(step_count, slots_here, query_width)
        .astype(jnp.bfloat16)
    )
    return (
        attended,
        landed_keys.reshape(1, fresh_span, kv_width),
        landed_values.reshape(1, fresh_span, kv_width),
    )


def solution(mesh):
    in_specs = (
        P(None, ("groups", "seq"), None),
        P(None, ("groups", "seq"), None),
        P(None, ("groups", "seq"), None),
        P(("groups", "seq"), None, None),
        P(("groups", "seq"), None, None),
        P(("groups", "seq"), None),
        P(("groups", "seq")),
        P(None, ("groups", "seq"), None, None),
        P(None, ("groups", "seq"), None, None),
        P("groups"),
        P("groups"),
    )
    out_specs = (
        P(None, ("groups", "seq"), None),
        P(("groups", "seq"), None, None),
        P(("groups", "seq"), None, None),
    )
    return jax.shard_map(
        per_device, mesh=mesh, in_specs=in_specs, out_specs=out_specs, check_vma=False
    )
```

profile of v0, /device:TPU:0, one launch (start us, length us, event | category | flops | bytes accessed | tf_op | source)
XLA Modules:
  0.0 74.1 jit_solution(8645931872850768993)
XLA Ops:
  0.6 1.8 %copy.177 = bf16[4,1,16,1024]{3,0,2,1:T(4,128)(2,1)} copy(bf16[4,1,16,1024]{3,2,1,0:T(8,128)(2,1)} %param.18) | data formatting | bytes 262144 | tf_op args[7]
  2.5 7.4 %all-to-all-start = ((bf16[4,16,1024]{2,0,1:T(4,128)(2,1)}), bf16[4,16,1024]{2,0,1:T(4,128)(2,1)S(1)}, u32[]{:S(2)}, u32[]{:S(2)}) async-start(bf16[4,16,1024]{2,0,1:T(4,128)(2,1)} %bitcast.87), calls=%async_computation | async-start | bytes 262144 | tf_op jit(solution)/shard_map/all_to_all | solution.py:45
  9.9 0.8 %reshape.284 = s32[64,1]{0,1:T(1,128)S(1)} reshape(s32[4,16]{1,0:T(4,128)} %param.16) | data formatting | bytes 512 | tf_op jit(solution)/shard_map/reshape | solution.py:83
  10.7 0.7 iota_compare_fusion.3
  11.4 1.3 %fusion.55 = (s32[]{:T(128)}, s32[]{:T(128)}, s32[16]{0:T(128)S(1)}, s32[16]{0:T(128)S(1)}) fusion(s32[]{:T(128)S(6)} %axis_index.12, s32[16]{0:T(128)} %param.21, s32[16]{0:T(128)} %param.20), kind=kLoop, calls=%fused_computation.83 | loop fusion | flops 638 | bytes 268 | tf_op jit(solution)/shard_map/reduce_sum | solution.py:39
  13.2 1.2 %reshape.287 = bf16[4,4,8,8,128]{4,3,2,1,0:T(8,128)(2,1)S(1)} reshape(bf16[4,4,8192]{2,1,0:T(4,128)(2,1)} %param.11) | data formatting | bytes 524288 | tf_op jit(solution)/shard_map/reshape | solution.py:82
  14.5 2.0 %gather_fusion.1 = bf16[64,16,1024]{2,1,0:T(8,128)(2,1)} fusion(bf16[64,16,1024]{2,1,0:T(8,128)(2,1)S(1)} %copy-done, s32[1024]{0:T(1024)S(1)} %pad_clamp_fusion), kind=kCustom, calls=%fused_computation.1 | custom fusion | bytes 4194560 | tf_op jit(solution)/shard_map/gather | solution.py:84
  16.5 2.2 %copy.126 = bf16[128,8,8,128]{3,2,1,0:T(8,128)(2,1)S(1)} copy(bf16[128,8,8,128]{3,1,2,0:T(8,128)(2,1)} %bitcast.93) | data formatting | bytes 4194304
  18.9 1.8 %fusion.58 = (f32[4,4,8,8]{3,0,2,1:T(4,128)S(1)}, f32[4,4,8,8,256]{4,3,0,2,1:T(8,128)}) fusion(bf16[4,4,8,8,128]{4,3,2,1,0:T(8,128)(2,1)S(1)} %reshape.287, bf16[4,256,8,128,1]{3,2,1,0,4:T(8,128)(2,1)S(1)} %bitcast_bitcast_fusion, pred[4,256]{1,0:T(4,128)(4,1)S(1)} %iota_compare_fusion.3), kind=kOutput, calls=%fused_computation.86 | convolution fusion | flops 67894272 | bytes 3412992 | tf_op jit(solution)/shard_map/srgeh,rcgh->srgec/dot_general | solution.py:88
  20.8 0.8 %copy.176 = bf16[4,1,16,1024]{3,0,2,1:T(4,128)(2,1)} copy(bf16[4,1,16,1024]{3,2,1,0:T(8,128)(2,1)S(1)} %copy-done.3) | data formatting | bytes 262144 | tf_op args[8]
  21.5 1.3 %fusion.59 = (f32[4,4,8,8]{3,0,2,1:T(4,128)S(1)}, f32[4,4,8,8,4]{3,4,0,2,1:T(4,128)S(1)}) fusion(bf16[4,4,8,8,128]{4,3,2,1,0:T(8,128)(2,1)S(1)} %reshape.287, bf16[4,4,8,128,1]{3,2,1,0,4:T(8,128)(2,1)S(1)} %bitcast.103, pred[4,4]{1,0:T(4,128)(4,1)S(1)} %iota_compare_fusion.4), kind=kOutput, calls=%fused_computation.87 | convolution fusion | flops 1059840 | bytes 315408 | tf_op jit(solution)/shard_map/srgeh,trgh->srget/dot_general | solution.py:98
  22.8 6.0 %all-to-all-start.2 = ((bf16[4,16,1024]{2,0,1:T(4,128)(2,1)}), bf16[4,16,1024]{2,0,1:T(4,128)(2,1)S(1)}, u32[]{:S(2)}, u32[]{:S(2)}) async-start(bf16[4,16,1024]{2,0,1:T(4,128)(2,1)} %bitcast.86), calls=%async_computation.2 | async-start | bytes 262144 | tf_op jit(solution)/shard_map/all_to_all | solution.py:46
  28.9 0.7 iota_compare_fusion.6
  31.0 3.6 %gather_fusion = bf16[64,16,1024]{2,1,0:T(8,128)(2,1)} fusion(bf16[64,16,1024]{2,1,0:T(8,128)(2,1)} %param.15, s32[1024]{0:T(1024)S(1)} %pad_clamp_fusion), kind=kCustom, calls=%fused_computation | custom fusion | bytes 4194560 | tf_op jit(solution)/shard_map/gather | solution.py:85
  34.6 3.6 %copy.125 = bf16[128,8,8,128]{3,2,1,0:T(8,128)(2,1)} copy(bf16[128,8,8,128]{3,1,2,0:T(8,128)(2,1)} %bitcast.92) | data formatting | bytes 4194304
  39.1 0.8 %reshape.293 = bf16[16,5,1024]{2,1,0:T(8,128)(2,1)} reshape(bf16[80,1024]{1,0:T(8,128)(2,1)S(1)} %convolution_convert_fusion.1) | data formatting | bytes 327680 | tf_op jit(solution)/shard_map/reshape | solution.py:66
  40.0 6.0 %all-to-all-start.1 = ((bf16[16,5,1024]{2,1,0:T(8,128)(2,1)}), bf16[16,5,1024]{2,1,0:T(8,128)(2,1)S(1)}, u32[]{:S(2)}, u32[]{:S(2)}) async-start(bf16[16,5,1024]{2,1,0:T(8,128)(2,1)} %reshape.293), calls=%async_computation.1 | async-start | bytes 524288 | tf_op jit(solution)/shard_map/all_to_all | solution.py:69
  46.9 0.8 %reshape.297 = bf16[16,5,1024]{2,1,0:T(8,128)(2,1)} reshape(bf16[80,1024]{1,0:T(8,128)(2,1)S(1)} %convolution_convert_fusion) | data formatting | bytes 327680 | tf_op jit(solution)/shard_map/reshape | solution.py:67
  47.7 8.3 %all-to-all-done.1 = bf16[16,5,1024]{2,1,0:T(8,128)(2,1)S(1)} async-done(((bf16[16,5,1024]{2,1,0:T(8,128)(2,1)}), bf16[16,5,1024]{2,1,0:T(8,128)(2,1)S(1)}, u32[]{:S(2)}, u32[]{:S(2)}) %all-to-all-start.1) | async-done | bytes 163872 | tf_op jit(solution)/shard_map/all_to_all | solution.py:69
  56.0 3.5 %all-to-all-start.3 = ((bf16[16,5,1024]{2,1,0:T(8,128)(2,1)}), bf16[16,5,1024]{2,1,0:T(8,128)(2,1)S(1)}, u32[]{:S(2)}, u32[]{:S(2)}) async-start(bf16[16,5,1024]{2,1,0:T(8,128)(2,1)} %reshape.297), calls=%async_computation.3 | async-start | bytes 524288 | tf_op jit(solution)/shard_map/all_to_all | solution.py:70
  59.5 3.0 %bitcast_bitcast_fusion.1 = bf16[4,256,8,128,1]{3,2,1,0,4:T(8,128)(2,1)} fusion(bf16[4,256,8,128]{3,2,1,0:T(8,128)(2,1)} %bitcast.90), kind=kLoop, calls=%fused_computation.3 | loop fusion | bytes 4194304 | tf_op jit(solution)/shard_map/reshape | solution.py:85
  62.7 6.8 %all-to-all-done.3 = bf16[16,5,1024]{2,1,0:T(8,128)(2,1)S(1)} async-done(((bf16[16,5,1024]{2,1,0:T(8,128)(2,1)}), bf16[16,5,1024]{2,1,0:T(8,128)(2,1)S(1)}, u32[]{:S(2)}, u32[]{:S(2)}) %all-to-all-start.3) | async-done | bytes 163872 | tf_op jit(solution)/shard_map/all_to_all | solution.py:70
  69.7 0.8 %bitcast_select_fusion.2 = (bf16[1,80,1024]{2,1,0:T(8,128)(2,1)}, bf16[1,80,1024]{2,1,0:T(8,128)(2,1)}) fusion(bf16[1,5,16,1024]{3,2,1,0:T(8,128)(2,1)S(1)} %copy.102, pred[80]{0:T(512)(128)(4,1)S(1)} %iota_compare_fusion.5, bf16[1,5,16,1024]{3,2,1,0:T(8,128)(2,1)S(1)} %copy.95), kind=kLoop, calls=%fused_computation.33 | loop fusion | flops 163840 | bytes 655440 | tf_op jit(solution)/shard_map/jit(_where)/select_n | solution.py:79
  73.3 0.8 %convert_element_type.19 = bf16[4,4,8192]{2,1,0:T(4,128)(2,1)} reshape(bf16[4,4,8,8,128]{4,3,2,1,0:T(8,128)(2,1)S(1)} %copy.104) | data formatting | bytes 524288 | tf_op jit(solution)/shard_map/convert_element_type | solution.py:132
  (52 shorter events, 5.2 us)
Async XLA Ops:
  0.6 13.9 %copy-start = (bf16[64,16,1024]{2,1,0:T(8,128)(2,1)S(1)}, bf16[64,16,1024]{2,1,0:T(8,128)(2,1)}, u32[]{:S(2)}) copy-start(bf16[64,16,1024]{2,1,0:T(8,128)(2,1)} %param.14) | copy-start | bytes 6291460
  2.5 20.4 %all-to-all-start = ((bf16[4,16,1024]{2,0,1:T(4,128)(2,1)}), bf16[4,16,1024]{2,0,1:T(4,128)(2,1)S(1)}, u32[]{:S(2)}, u32[]{:S(2)}) async-start(bf16[4,16,1024]{2,0,1:T(4,128)(2,1)} %bitcast.87), calls=%async_computation | async-start | bytes 262144 | tf_op jit(solution)/shard_map/all_to_all | solution.py:45
  18.9 1.8 %copy-start.4 = (bf16[4,4,1024]{2,1,0:T(4,128)(2,1)S(1)}, bf16[4,4,1024]{2,1,0:T(4,128)(2,1)}, u32[]{:S(2)}) copy-start(bf16[4,4,1024]{2,1,0:T(4,128)(2,1)} %param.12) | copy-start | bytes 98308
  18.9 1.9 %copy-start.3 = (bf16[4,1,16,1024]{3,2,1,0:T(8,128)(2,1)S(1)}, bf16[4,1,16,1024]{3,2,1,0:T(8,128)(2,1)}, u32[]{:S(2)}) copy-start(bf16[4,1,16,1024]{3,2,1,0:T(8,128)(2,1)} %param.19) | copy-start | bytes 393220
  18.9 12.1 %copy-start.5 = (bf16[4,4,1024]{2,1,0:T(4,128)(2,1)S(1)}, bf16[4,4,1024]{2,1,0:T(4,128)(2,1)}, u32[]{:S(2)}) copy-start(bf16[4,4,1024]{2,1,0:T(4,128)(2,1)} %param.13) | copy-start | bytes 98308
  22.8 17.1 %all-to-all-start.2 = ((bf16[4,16,1024]{2,0,1:T(4,128)(2,1)}), bf16[4,16,1024]{2,0,1:T(4,128)(2,1)S(1)}, u32[]{:S(2)}, u32[]{:S(2)}) async-start(bf16[4,16,1024]{2,0,1:T(4,128)(2,1)} %bitcast.86), calls=%async_computation.2 | async-start | bytes 262144 | tf_op jit(solution)/shard_map/all_to_all | solution.py:46
  40.0 16.0 %all-to-all-start.1 = ((bf16[16,5,1024]{2,1,0:T(8,128)(2,1)}), bf16[16,5,1024]{2,1,0:T(8,128)(2,1)S(1)}, u32[]{:S(2)}, u32[]{:S(2)}) async-start(bf16[16,5,1024]{2,1,0:T(8,128)(2,1)} %reshape.293), calls=%async_computation.1 | async-start | bytes 524288 | tf_op jit(solution)/shard_map/all_to_all | solution.py:69
  56.0 13.5 %all-to-all-start.3 = ((bf16[16,5,1024]{2,1,0:T(8,128)(2,1)}), bf16[16,5,1024]{2,1,0:T(8,128)(2,1)S(1)}, u32[]{:S(2)}, u32[]{:S(2)}) async-start(bf16[16,5,1024]{2,1,0:T(8,128)(2,1)} %reshape.297), calls=%async_computation.3 | async-start | bytes 524288 | tf_op jit(solution)/shard_map/all_to_all | solution.py:70
  69.5 2.3 %copy-start.2 = (f32[4,4,8,8,256]{4,3,0,2,1:T(8,128)S(1)}, f32[4,4,8,8,256]{4,3,0,2,1:T(8,128)}, u32[]{:S(2)}) copy-start(f32[4,4,8,8,256]{4,3,0,2,1:T(8,128)} %get-tuple-element.14) | copy-start | bytes 3145732
  70.7 2.0 %copy-start.1 = (bf16[4,256,8,128,1]{3,2,1,0,4:T(8,128)(2,1)S(1)}, bf16[4,256,8,128,1]{3,2,1,0,4:T(8,128)(2,1)}, u32[]{:S(2)}) copy-start(bf16[4,256,8,128,1]{3,2,1,0,4:T(8,128)(2,1)} %bitcast_bitcast_fusion.1) | copy-start | bytes 6291460
where the time goes:
time: 74.8 us; the launch traced here: 74.1 us
  starting transfers between devices  23 us (31%)
  local copies, waits for them, and re-layouts  22.2 us (30%)
  waiting for transfers between devices  15.1 us (20%)
  other arithmetic  5.9 us (8%)
  matrix products  4.96 us (7%)
  between operations  2.9 us (4%)
    unnamed x18, local copies, waits for them, and re-layouts  8.44 us
    all_to_all x1, waiting for transfers between devices, per_device(): lax.all_to_all(send_keys, 'seq', split_axis=0, concat_axis=2, tiled=True)  8.3 us
    all_to_all x1, starting transfers between devices, per_device(): lax.all_to_all(local_keys, 'seq', split_axis=1, concat_axis=1, tiled=True)  7.41 us
    all_to_all x1, waiting for transfers between devices, per_device(): lax.all_to_all(send_values, 'seq', split_axis=0, concat_axis=2, tiled=True)  6.84 us
    all_to_all x1, starting transfers between devices, per_device(): lax.all_to_all(local_values, 'seq', split_axis=1, concat_axis=1, tiled=True)  6.01 us
    all_to_all x1, starting transfers between devices, per_device(): lax.all_to_all(send_keys, 'seq', split_axis=0, concat_axis=2, tiled=True)  6.01 us
    gather x1, local copies, waits for them, and re-layouts, per_device(): resident_values = pool_values[pool_rows].reshape(slots_here, -1, KVH, HD)  3.57 us
    all_to_all x1, starting transfers between devices, per_device(): lax.all_to_all(send_values, 'seq', split_axis=0, concat_axis=2, tiled=True)  3.53 us
  transfers between devices with their start and end apart: 4, of which 2 were waited for; matrix products, arithmetic and copies ran while one was open for 36% of the time, Pallas kernels for 0%

commit v1 on v0

v1 whole, which is shorter than its diff:
```python
import functools
import math

import jax
import jax.numpy as jnp
from jax import lax
from jax.experimental import pallas as pl
from jax.experimental.pallas import tpu as pltpu
from jax.sharding import PartitionSpec as P

QH = 64
KVH = 8
HD = 128
MOSTT = 80
SUB = 8
LANES = 128
NEG = -1e30
F32 = jnp.float32
BF16 = jnp.bfloat16


def kernel(
    n,
    table_ref,
    cached_ref,
    lengths_ref,
    slots_ref,
    q_hbm,
    nk_hbm,
    nv_hbm,
    pk_hbm,
    pv_hbm,
    tk_hbm,
    tv_hbm,
    out_ref,
    lk_ref,
    lv_ref,
    q_v,
    n_v,
    pk_v,
    pv_v,
    t_v,
    first_k,
    first_v,
    second,
    landing_k,
    landing_v,
    fresh,
    qf,
    of,
    acc,
    mx,
    sm,
    start_s,
    pick_s,
    load_sem,
    own_sem,
    send1,
    recv1,
    send2,
    recv2,
):
    me = lax.axis_index("seq")
    steps, slots_here, _ = q_hbm.shape
    group_pages, page_rows, kv_width = tk_hbm.shape
    pages_here = pk_hbm.shape[0]
    turns = lengths_ref.shape[0]
    cache_pages = table_ref.shape[1]
    lane_tiles = kv_width // LANES
    spread = (page_rows // SUB) * lane_tiles
    most_pages = -(-MOSTT // page_rows)
    fresh_span = most_pages * page_rows
    blocks = n // spread
    share = QH // KVH
    rows_sr = steps * slots_here
    my_block = me // spread
    first = (first_k, first_v)
    landing = (landing_k, landing_v)

    def load(index, src, dst):
        return pltpu.make_async_copy(src, dst, load_sem.at[index])

    loads = [
        load(0, tk_hbm, t_v.at[0]),
        load(1, tv_hbm, t_v.at[1]),
        load(2, q_hbm, q_v),
        load(3, pk_hbm, pk_v),
        load(4, pv_hbm, pv_v),
        load(5, nk_hbm, n_v.at[0]),
        load(6, nv_hbm, n_v.at[1]),
    ]
    for copy in loads:
        copy.start()

    barrier = pltpu.get_barrier_semaphore()

    @pl.loop(1, n)
    def _(k):
        pl.semaphore_signal(barrier, inc=1, device_id={"seq": lax.rem(me + k, n)})

    running = jnp.int32(0)
    my_length = jnp.int32(0)
    my_slot = jnp.int32(0)
    for t in range(turns):
        start_s[t] = running
        length = lengths_ref[t]
        slot = slots_ref[t]
        mine = lax.div(slot, slots_here) == me
        my_length = jnp.where(mine, length, my_length)
        my_slot = jnp.where(mine, lax.rem(slot, slots_here), my_slot)
        running = running + lax.div(length + (page_rows - 1), page_rows)

    @pl.loop(0, n)
    def _(d):
        begin = jnp.int32(0)
        for t in range(turns):
            begin = jnp.where(lax.div(slots_ref[t], slots_here) == d, start_s[t], begin)
        for j in range(most_pages):
            page = jnp.minimum(begin + j, group_pages * n - 1)
            row = lax.rem(lax.rem(page, n), spread) * group_pages + lax.div(page, n)
            pick_s[d * most_pages + j] = row

    def tile(h):
        t = lax.rem(h, spread)
        top = pl.multiple_of(lax.div(t, lane_tiles) * SUB, SUB)
        left = pl.multiple_of(lax.rem(t, lane_tiles) * LANES, LANES)
        return pl.ds(top, SUB), pl.ds(left, LANES)

    def slot_of(src):
        return pl.ds(lax.rem(src, spread) * group_pages, group_pages)

    def hand1(a, k):
        h = my_block * spread + lax.rem(lax.rem(me, spread) + k, spread)
        top, left = tile(h)
        return pltpu.make_async_remote_copy(
            src_ref=t_v.at[a, :, top, left],
            dst_ref=first[a].at[slot_of(me)],
            send_sem=send1.at[a, k],
            recv_sem=recv1.at[a, k],
            device_id={"seq": h},
        )

    def own1(a):
        top, left = tile(me)
        return pltpu.make_async_copy(
            t_v.at[a, :, top, left], first[a].at[slot_of(me)], own_sem.at[a]
        )

    def hand2(a, k):
        d = lax.rem(me + k, n)
        top, left = tile(me)
        return pltpu.make_async_remote_copy(
            src_ref=second.at[a, pl.ds(d * most_pages, most_pages)],
            dst_ref=landing[a].at[pl.ds(my_block * most_pages, most_pages), top, left],
            send_sem=send2.at[a, k],
            recv_sem=recv2.at[a, k],
            device_id={"seq": d},
        )

    def own2(a):
        top, left = tile(me)
        return pltpu.make_async_copy(
            second.at[a, pl.ds(me * most_pages, most_pages)],
            landing[a].at[pl.ds(my_block * most_pages, most_pages), top, left],
            own_sem.at[2 + a],
        )

    loads[0].wait()
    loads[1].wait()
    pl.semaphore_wait(barrier, n - 1)
    for a in range(2):

        @pl.loop(1, spread)
        def _(k, a=a):
            hand1(a, k).start()

        own1(a).start()

    loads[2].wait()
    for s in range(steps):
        qf[pl.ds(s * slots_here, slots_here), :] = q_v[s].astype(F32)

    tokens = pages_here * page_rows
    col = lax.broadcasted_iota(jnp.int32, (1, tokens), 1)
    col_page = col // page_rows
    col_row = col % page_rows
    lines = []
    for r in range(slots_here):
        room = jnp.zeros((1, tokens), jnp.int32)
        for c in range(cache_pages):
            left_over = cached_ref[r] - c * page_rows
            room = jnp.where(col_page == table_ref[r, c], left_over, room)
        lines.append(jnp.where(col_row < room, 0.0, NEG).astype(F32))
    bias = jnp.concatenate(lines * (rows_sr // slots_here), axis=0)
    factor = math.log2(math.e) / math.sqrt(HD)

    def group_queries(g):
        parts = [qf[:, pl.ds((g * share + e) * HD, HD)] for e in range(share)]
        return jnp.concatenate(parts, axis=0).astype(BF16)

    def scores_of(g, keys, biases):
        raw = lax.dot_general(
            group_queries(g), keys, (((1,), (1,)), ((), ())), preferred_element_type=F32
        )
        shaped = raw.reshape(share, rows_sr, keys.shape[0]) * factor + biases[None]
        return shaped.reshape(share * rows_sr, keys.shape[0])

    def resident(g):
        keys = pk_v[:, :, pl.ds(g * HD, HD)].reshape(tokens, HD)
        values = pv_v[:, :, pl.ds(g * HD, HD)].reshape(tokens, HD)
        score = scores_of(g, keys, bias)
        largest = jnp.max(score, axis=-1, keepdims=True)
        prob = jnp.exp2(score - largest)
        mx[g] = jnp.broadcast_to(largest, mx.shape[1:])
        sm[g] = jnp.broadcast_to(jnp.sum(prob, axis=-1, keepdims=True), sm.shape[1:])
        acc[g] = jnp.dot(prob.astype(BF16), values, preferred_element_type=F32)

    loads[3].wait()
    loads[4].wait()
    half = KVH // 2
    for g in range(half):
        resident(g)

    for a in range(2):

        @pl.loop(1, spread)
        def _(k, a=a):
            hand1(a, k).wait_recv()

        own1(a).wait()
        for i in range(n * most_pages):
            second[a, i] = first[a][pick_s[i]]

        @pl.loop(1, n)
        def _(k, a=a):
            hand2(a, k).start()

        own2(a).start()

    for g in range(half, KVH):
        resident(g)

    loads[5].wait()
    loads[6].wait()
    for a in range(2):
        fresh[a, most_pages] = jnp.concatenate(
            [n_v[a, s].astype(F32) for s in range(steps)], axis=0
        ).astype(BF16)
    extra = fresh_span + rows_sr
    line = lax.broadcasted_iota(jnp.int32, (rows_sr, extra), 0)
    col = lax.broadcasted_iota(jnp.int32, (rows_sr, extra), 1)
    line_slot, line_step = line % slots_here, line // slots_here
    new_at = jnp.maximum(col - fresh_span, 0)
    fine_fresh = (line_slot == my_slot) & (col < my_length)
    fine_new = (
        (col >= fresh_span)
        & (new_at % slots_here == line_slot)
        & (new_at // slots_here <= line_step)
    )
    bias2 = jnp.where(fine_fresh | fine_new, 0.0, NEG).astype(F32)

    place = lax.broadcasted_iota(jnp.int32, (page_rows, kv_width), 0)
    landed = (lk_ref, lv_ref)
    for a in range(2):

        @pl.loop(1, n)
        def _(k, a=a):
            hand2(a, k).wait_recv()

        own2(a).wait()
        for j in range(most_pages):
            if blocks == 1:
                block = 0
            else:
                begin = jnp.int32(0)
                for t in range(turns):
                    begin = jnp.where(
                        lax.div(slots_ref[t], slots_here) == me, start_s[t], begin
                    )
                block = lax.div(lax.rem(jnp.minimum(begin + j, group_pages * n - 1), n), spread)
            page = landing[a][block * most_pages + j]
            kept = jnp.where(place + j * page_rows < my_length, page.astype(F32), 0.0)
            kept = kept.astype(BF16)
            fresh[a, j] = kept
            landed[a][j] = kept

    for g in range(KVH):
        keys = fresh[0, :, :, pl.ds(g * HD, HD)].reshape(extra, HD)
        values = fresh[1, :, :, pl.ds(g * HD, HD)].reshape(extra, HD)
        score = scores_of(g, keys, bias2)
        before = mx[g]
        largest = jnp.maximum(before, jnp.max(score, axis=-1, keepdims=True))
        prob = jnp.exp2(score - largest[:, :extra])
        shrink = jnp.exp2(before - largest)
        total = sm[g] * shrink + jnp.sum(prob, axis=-1, keepdims=True)
        mixed = acc[g] * shrink + jnp.dot(
            prob.astype(BF16), values, preferred_element_type=F32
        )
        result = mixed / total
        for e in range(share):
            of[:, pl.ds((g * share + e) * HD, HD)] = result[e * rows_sr : (e + 1) * rows_sr]
    for s in range(steps):
        out_ref[s] = of[pl.ds(s * slots_here, slots_here), :].astype(BF16)

    for a in range(2):

        @pl.loop(1, spread)
        def _(k, a=a):
            hand1(a, k).wait_send()

        @pl.loop(1, n)
        def _(k, a=a):
            hand2(a, k).wait_send()


def per_device(
    queries,
    new_keys,
    new_values,
    pool_keys,
    pool_values,
    page_table,
    cached_len,
    turn_keys,
    turn_values,
    turn_lengths,
    turn_slot,
):
    n = lax.axis_size("seq")
    steps, slots_here, query_width = queries.shape
    pages_here, page_rows, kv_width = pool_keys.shape
    group_pages = turn_keys.shape[0]
    most_pages = -(-MOSTT // page_rows)
    spread = (page_rows // SUB) * (kv_width // LANES)
    blocks = n // spread
    rows_sr = steps * slots_here
    rows = rows_sr * (QH // KVH)
    paged = (group_pages, page_rows, kv_width)
    smem = pl.BlockSpec(memory_space=pltpu.SMEM)
    anywhere = pl.BlockSpec(memory_space=pl.ANY)
    vmem = pl.BlockSpec(memory_space=pltpu.VMEM)
    landed = jax.ShapeDtypeStruct((most_pages, page_rows, kv_width), BF16)
    attended, landed_keys, landed_values = pl.pallas_call(
        functools.partial(kernel, n),
        out_shape=(jax.ShapeDtypeStruct(queries.shape, BF16), landed, landed),
        in_specs=[smem] * 4 + [anywhere] * 7,
        out_specs=(vmem, vmem, vmem),
        scratch_shapes=[
            pltpu.VMEM(queries.shape, BF16),
            pltpu.VMEM((2,) + new_keys.shape, BF16),
            pltpu.VMEM(pool_keys.shape, BF16),
            pltpu.VMEM(pool_values.shape, BF16),
            pltpu.VMEM((2,) + paged, BF16),
            pltpu.VMEM((spread * group_pages, SUB, LANES), BF16),
            pltpu.VMEM((spread * group_pages, SUB, LANES), BF16),
            pltpu.VMEM((2, n * most_pages, SUB, LANES), BF16),
            pltpu.VMEM((blocks * most_pages, page_rows, kv_width), BF16),
            pltpu.VMEM((blocks * most_pages, page_rows, kv_width), BF16),
            pltpu.VMEM((2, most_pages + 1, page_rows, kv_width), BF16),
            pltpu.VMEM((rows_sr, query_width), F32),
            pltpu.VMEM((rows_sr, query_width), F32),
            pltpu.VMEM((KVH, rows, HD), F32),
            pltpu.VMEM((KVH, rows, HD), F32),
            pltpu.VMEM((KVH, rows, HD), F32),
            pltpu.SMEM(turn_lengths.shape, jnp.int32),
            pltpu.SMEM((n * most_pages,), jnp.int32),
            pltpu.SemaphoreType.DMA((7,)),
            pltpu.SemaphoreType.DMA((4,)),
            pltpu.SemaphoreType.DMA((2, spread)),
            pltpu.SemaphoreType.DMA((2, spread)),
            pltpu.SemaphoreType.DMA((2, n)),
            pltpu.SemaphoreType.DMA((2, n)),
        ],
        compiler_params=pltpu.CompilerParams(
            collective_id=0, has_side_effects=True, vmem_limit_bytes=60 * 1024 * 1024
        ),
    )(
        page_table,
        cached_len,
        turn_lengths,
        turn_slot,
        queries,
        new_keys,
        new_values,
        pool_keys,
        pool_values,
        turn_keys.reshape(paged),
        turn_values.reshape(paged),
    )
    span = most_pages * page_rows
    return (
        attended,
        landed_keys.reshape(1, span, kv_width),
        landed_values.reshape(1, span, kv_width),
    )


def solution(mesh):
    in_specs = (
        P(None, ("groups", "seq"), None),
        P(None, ("groups", "seq"), None),
        P(None, ("groups", "seq"), None),
        P(("groups", "seq"), None, None),
        P(("groups", "seq"), None, None),
        P(("groups", "seq"), None),
        P(("groups", "seq")),
        P(None, ("groups", "seq"), None, None),
        P(None, ("groups", "seq"), None, None),
        P("groups"),
        P("groups"),
    )
    out_specs = (
        P(None, ("groups", "seq"), None),
        P(("groups", "seq"), None, None),
        P(("groups", "seq"), None, None),
    )
    return jax.shard_map(
        per_device, mesh=mesh, in_specs=in_specs, out_specs=out_specs, check_vma=False
    )
```

time: 74.8 us -> 29.9 us (0.40)
  Pallas kernels: 0 us -> 24.1 us
  starting transfers between devices: 23 us -> 0 us
  local copies, waits for them, and re-layouts: 22.2 us -> 4.93 us
  waiting for transfers between devices: 15.1 us -> 0 us
  other arithmetic: 5.9 us -> 0 us
  matrix products: 4.96 us -> 0 us
  between operations: 2.9 us -> 0.64 us
    pallas_call x0 -> x1, Pallas kernels: none -> 24.1 us  [per_device(): pl.pallas_call(functools.partial(kernel, n), out_shape=(jax.ShapeDtypeStr...]
    all_to_all x4 -> x0, starting transfers between devices: 23 us -> none  [the longest x1 7.41 us: per_device(): lax.all_to_all(local_keys, 'seq', split_axis=1, concat_axis=1, tiled=True)]
    all_to_all x4 -> x0, waiting for transfers between devices: 15.1 us -> none  [the longest x1 8.3 us: per_device(): lax.all_to_all(send_keys, 'seq', split_axis=0, concat_axis=2, tiled=True)]
    reshape x8 -> x0, local copies, waits for them, and re-layouts: 6.78 us -> none  [the longest x1 3.02 us: per_device(): resident_values = pool_values[pool_rows].reshape(slots_here, -1, KVH, HD)]
    gather x2 -> x0, local copies, waits for them, and re-layouts: 5.6 us -> none  [the longest x1 3.57 us: per_device(): resident_values = pool_values[pool_rows].reshape(slots_here, -1, KVH, HD)]
    dot_general x8 -> x0, matrix products: 4.96 us -> none  [the longest x1 1.79 us: per_device(): jnp.einsum('srgeh,rcgh->srgec', query_heads, resident_keys, preferred_ele...]
    unnamed x18 -> x3, local copies, waits for them, and re-layouts: 8.44 us -> 4.93 us
    reduce_sum x5 -> x0, other arithmetic: 2.38 us -> none  [the longest x1 1.35 us: per_device(): my_slot = jnp.sum(jnp.where(owned, turn_slot % slots_here, 0))]
  transfers between devices with their start and end apart: 4 -> 0, of which waited for: 2 -> 0; matrix products, arithmetic and copies ran while one was open for 36% -> 0% of each run, Pallas kernels for 0% -> 0%
where the time goes in v1:
time: 29.9 us; the launch traced here: 29.7 us
  Pallas kernels  24.1 us (81%)
  local copies, waits for them, and re-layouts  4.93 us (16%)
  between operations  0.64 us (2%)
    pallas_call x1, Pallas kernels, per_device(): pl.pallas_call(functools.partial(kernel, n), out_shape=(jax.ShapeDtypeStr...  24.1 us
    unnamed x3, local copies, waits for them, and re-layouts  4.93 us

profile of v1, /device:TPU:0, one launch (start us, length us, event | category | flops | bytes accessed | tf_op | source)
XLA Modules:
  0.0 29.7 jit_solution(11746131278769919244)
XLA Ops:
  0.6 24.1 %shard_map.130 = (bf16[4,4,8192]{2,1,0:T(4,128)(2,1)}, bf16[5,16,1024]{2,1,0:T(8,128)(2,1)}, bf16[5,16,1024]{2,1,0:T(8,128)(2,1)}) custom-call(s32[4,16]{1,0:T(4,128)} %table_ref.1, s32[4]{0:T(128)} %cached_ref.1, s32[16]{0:T(128)} %lengths_ref.1, s32[16]{0:T(128)} %slots_ref.1, bf16[4,4,8192]{2,1,0:T(4,128)(2,1)} %q_hbm.1, bf16[4,4,1024]{2,1,0:T(4,128)(2,1)} %nk_hbm.1, ...), custom_call_target="tpu_custom_call" | custom-call | tf_op jit(solution)/shard_map/pallas_call | solution.py:343
  24.8 1.7 %copy.17 = bf16[4,4,8192]{2,1,0:T(4,128)(2,1)} copy(bf16[4,4,8192]{2,1,0:T(4,128)(2,1)} %get-tuple-element.12) | data formatting | bytes 524288
  26.5 1.6 %copy.18 = bf16[1,80,1024]{2,1,0:T(8,128)(2,1)} copy(bf16[1,80,1024]{2,1,0:T(8,128)(2,1)} %bitcast.5) | data formatting | bytes 327680
  28.1 1.6 %copy.19 = bf16[1,80,1024]{2,1,0:T(8,128)(2,1)} copy(bf16[1,80,1024]{2,1,0:T(8,128)(2,1)} %bitcast.4) | data formatting | bytes 327680

commit v2 on v1

--- a/solution.py
+++ b/solution.py
@@ -17,6 +17,101 @@
 NEG = -1e30
 F32 = jnp.float32
 BF16 = jnp.bfloat16
+
+
+FACTOR = math.log2(math.e) / math.sqrt(HD)
+
+
+def scores_of(qb, g, keys, biases):
+    share = QH // KVH
+    parts = [qb[:, pl.ds((g * share + e) * HD, HD)] for e in range(share)]
+    rows = jnp.concatenate(parts, axis=0)
+    raw = lax.dot_general(rows, keys, (((1,), (1,)), ((), ())), preferred_element_type=F32)
+    shaped = raw.reshape(share, biases.shape[0], keys.shape[0]) * FACTOR + biases[None]
+    return shaped.reshape(rows.shape[0], keys.shape[0])
+
+
+def each(first, last):
+    if last - first > 32:
+        return pl.loop(first, last)
+
+    def run(body):
+        for k in range(first, last):
+            body(k)
+
+    return run
+
+
+def finish(
+    qb_hbm,
+    acc_hbm,
+    mx_hbm,
+    sm_hbm,
+    fresh_hbm,
+    bias2_hbm,
+    out_ref,
+    lk_hbm,
+    lv_hbm,
+    qb,
+    acc,
+    mx,
+    sm,
+    fresh,
+    bias2_ref,
+    of,
+    load_sem,
+    sem,
+):
+    loads = [
+        pltpu.make_async_copy(src, dst, load_sem.at[i])
+        for i, (src, dst) in enumerate(
+            (
+                (fresh_hbm.at[0], fresh.at[0]),
+                (fresh_hbm.at[1], fresh.at[1]),
+                (qb_hbm, qb),
+                (bias2_hbm, bias2_ref),
+                (mx_hbm, mx),
+                (sm_hbm, sm),
+                (acc_hbm, acc),
+            )
+        )
+    ]
+    for copy in loads:
+        copy.start()
+    share = QH // KVH
+    most_pages = lk_hbm.shape[0]
+    rows_sr = qb.shape[0]
+    steps, slots_here, _ = out_ref.shape
+    extra = bias2_ref.shape[1]
+    copies = [
+        pltpu.make_async_copy(fresh.at[a, pl.ds(0, most_pages)], ref, sem.at[a])
+        for a, ref in enumerate((lk_hbm, lv_hbm))
+    ]
+    for load, copy in zip(loads, copies):
+        load.wait()
+        copy.start()
+    for load in loads[2:]:
+        load.wait()
+    bias2 = bias2_ref[...]
+    for g in range(KVH):
+        keys = fresh[0, :, :, pl.ds(g * HD, HD)].reshape(extra, HD)
+        values = fresh[1, :, :, pl.ds(g * HD, HD)].reshape(extra, HD)
+        score = scores_of(qb, g, keys, bias2)
+        before = mx[:, g : g + 1]
+        largest = jnp.maximum(before, jnp.max(score, axis=-1, keepdims=True))
+        prob = jnp.exp2(score - largest)
+        shrink = jnp.exp2(before - largest)
+        total = sm[:, g : g + 1] * shrink + jnp.sum(prob, axis=-1, keepdims=True)
+        mixed = acc[g] * shrink + jnp.dot(
+            prob.astype(BF16), values, preferred_element_type=F32
+        )
+        result = mixed / total
+        for e in range(share):
+            of[:, pl.ds((g * share + e) * HD, HD)] = result[e * rows_sr : (e + 1) * rows_sr]
+    for s in range(steps):
+        out_ref[s] = of[pl.ds(s * slots_here, slots_here), :].astype(BF16)
+    for copy in copies:
+        copy.wait()
 
 
 def kernel(
@@ -32,9 +127,18 @@
     pv_hbm,
     tk_hbm,
     tv_hbm,
-    out_ref,
-    lk_ref,
-    lv_ref,
+    qb_hbm,
+    acc_hbm,
+    mx_hbm,
+    sm_hbm,
+    fresh_hbm,
+    bias2_hbm,
+    qb,
+    acc,
+    mx,
+    sm,
+    fresh,
+    bias2_ref,
     q_v,
     n_v,
     pk_v,
@@ -45,15 +149,11 @@
     second,
     landing_k,
     landing_v,
-    fresh,
     qf,
-    of,
-    acc,
-    mx,
-    sm,
     start_s,
     pick_s,
     load_sem,
+    out_sem,
     own_sem,
     send1,
     recv1,
@@ -71,11 +171,16 @@
     most_pages = -(-MOSTT // page_rows)
     fresh_span = most_pages * page_rows
     blocks = n // spread
-    share = QH // KVH
     rows_sr = steps * slots_here
     my_block = me // spread
     first = (first_k, first_v)
     landing = (landing_k, landing_v)
+
+    barrier = pltpu.get_barrier_semaphore()
+
+    @each(1, n)
+    def _(k):
+        pl.semaphore_signal(barrier, inc=1, device_id={"seq": lax.rem(me + k, n)})
 
     def load(index, src, dst):
         return pltpu.make_async_copy(src, dst, load_sem.at[index])
@@ -92,12 +197,6 @@
     for copy in loads:
         copy.start()
 
-    barrier = pltpu.get_barrier_semaphore()
-
-    @pl.loop(1, n)
-    def _(k):
-        pl.semaphore_signal(barrier, inc=1, device_id={"seq": lax.rem(me + k, n)})
-
     running = jnp.int32(0)
     my_length = jnp.int32(0)
     my_slot = jnp.int32(0)
@@ -170,7 +269,7 @@
     pl.semaphore_wait(barrier, n - 1)
     for a in range(2):
 
-        @pl.loop(1, spread)
+        @each(1, spread)
         def _(k, a=a):
             hand1(a, k).start()
 
@@ -179,6 +278,7 @@
     loads[2].wait()
     for s in range(steps):
         qf[pl.ds(s * slots_here, slots_here), :] = q_v[s].astype(F32)
+    qb[...] = qf[...].astype(BF16)
 
     tokens = pages_here * page_rows
     col = lax.broadcasted_iota(jnp.int32, (1, tokens), 1)
@@ -192,27 +292,14 @@
             room = jnp.where(col_page == table_ref[r, c], left_over, room)
         lines.append(jnp.where(col_row < room, 0.0, NEG).astype(F32))
     bias = jnp.concatenate(lines * (rows_sr // slots_here), axis=0)
-    factor = math.log2(math.e) / math.sqrt(HD)
-
-    def group_queries(g):
-        parts = [qf[:, pl.ds((g * share + e) * HD, HD)] for e in range(share)]
-        return jnp.concatenate(parts, axis=0).astype(BF16)
-
-    def scores_of(g, keys, biases):
-        raw = lax.dot_general(
-            group_queries(g), keys, (((1,), (1,)), ((), ())), preferred_element_type=F32
-        )
-        shaped = raw.reshape(share, rows_sr, keys.shape[0]) * factor + biases[None]
-        return shaped.reshape(share * rows_sr, keys.shape[0])
-
     def resident(g):
         keys = pk_v[:, :, pl.ds(g * HD, HD)].reshape(tokens, HD)
         values = pv_v[:, :, pl.ds(g * HD, HD)].reshape(tokens, HD)
-        score = scores_of(g, keys, bias)
+        score = scores_of(qb, g, keys, bias)
         largest = jnp.max(score, axis=-1, keepdims=True)
         prob = jnp.exp2(score - largest)
-        mx[g] = jnp.broadcast_to(largest, mx.shape[1:])
-        sm[g] = jnp.broadcast_to(jnp.sum(prob, axis=-1, keepdims=True), sm.shape[1:])
+        mx[:, g : g + 1] = largest
+        sm[:, g : g + 1] = jnp.sum(prob, axis=-1, keepdims=True)
         acc[g] = jnp.dot(prob.astype(BF16), values, preferred_element_type=F32)
 
     loads[3].wait()
@@ -223,7 +310,7 @@
 
     for a in range(2):
 
-        @pl.loop(1, spread)
+        @each(1, spread)
         def _(k, a=a):
             hand1(a, k).wait_recv()
 
@@ -231,7 +318,7 @@
         for i in range(n * most_pages):
             second[a, i] = first[a][pick_s[i]]
 
-        @pl.loop(1, n)
+        @each(1, n)
         def _(k, a=a):
             hand2(a, k).start()
 
@@ -257,13 +344,29 @@
         & (new_at % slots_here == line_slot)
         & (new_at // slots_here <= line_step)
     )
-    bias2 = jnp.where(fine_fresh | fine_new, 0.0, NEG).astype(F32)
+    bias2_ref[...] = jnp.where(fine_fresh | fine_new, 0.0, NEG).astype(F32)
+
+    stores = [
+        pltpu.make_async_copy(src, dst, out_sem.at[i])
+        for i, (src, dst) in enumerate(
+            (
+                (qb, qb_hbm),
+                (acc, acc_hbm),
+                (mx, mx_hbm),
+                (sm, sm_hbm),
+                (bias2_ref, bias2_hbm),
+                (fresh.at[0], fresh_hbm.at[0]),
+                (fresh.at[1], fresh_hbm.at[1]),
+            )
+        )
+    ]
+    for copy in stores[:5]:
+        copy.start()
 
     place = lax.broadcasted_iota(jnp.int32, (page_rows, kv_width), 0)
-    landed = (lk_ref, lv_ref)
     for a in range(2):
 
-        @pl.loop(1, n)
+        @each(1, n)
         def _(k, a=a):
             hand2(a, k).wait_recv()
 
@@ -280,37 +383,21 @@
                 block = lax.div(lax.rem(jnp.minimum(begin + j, group_pages * n - 1), n), spread)
             page = landing[a][block * most_pages + j]
             kept = jnp.where(place + j * page_rows < my_length, page.astype(F32), 0.0)
-            kept = kept.astype(BF16)
-            fresh[a, j] = kept
-            landed[a][j] = kept
-
-    for g in range(KVH):
-        keys = fresh[0, :, :, pl.ds(g * HD, HD)].reshape(extra, HD)
-        values = fresh[1, :, :, pl.ds(g * HD, HD)].reshape(extra, HD)
-        score = scores_of(g, keys, bias2)
-        before = mx[g]
-        largest = jnp.maximum(before, jnp.max(score, axis=-1, keepdims=True))
-        prob = jnp.exp2(score - largest[:, :extra])
-        shrink = jnp.exp2(before - largest)
-        total = sm[g] * shrink + jnp.sum(prob, axis=-1, keepdims=True)
-        mixed = acc[g] * shrink + jnp.dot(
-            prob.astype(BF16), values, preferred_element_type=F32
-        )
-        result = mixed / total
-        for e in range(share):
-            of[:, pl.ds((g * share + e) * HD, HD)] = result[e * rows_sr : (e + 1) * rows_sr]
-    for s in range(steps):
-        out_ref[s] = of[pl.ds(s * slots_here, slots_here), :].astype(BF16)
+            fresh[a, j] = kept.astype(BF16)
+        stores[5 + a].start()
 
     for a in range(2):
 
-        @pl.loop(1, spread)
+        @each(1, spread)
         def _(k, a=a):
             hand1(a, k).wait_send()
 
-        @pl.loop(1, n)
+        @each(1, n)
         def _(k, a=a):
             hand2(a, k).wait_send()
+
+    for copy in stores:
+        copy.wait()
 
 
 def per_device(
@@ -337,15 +424,28 @@
     rows = rows_sr * (QH // KVH)
     paged = (group_pages, page_rows, kv_width)
     smem = pl.BlockSpec(memory_space=pltpu.SMEM)
-    anywhere = pl.BlockSpec(memory_space=pl.ANY)
+    hbm = pl.BlockSpec(memory_space=pltpu.HBM)
     vmem = pl.BlockSpec(memory_space=pltpu.VMEM)
-    landed = jax.ShapeDtypeStruct((most_pages, page_rows, kv_width), BF16)
-    attended, landed_keys, landed_values = pl.pallas_call(
+    extra = most_pages * page_rows + rows_sr
+    parts = pl.pallas_call(
         functools.partial(kernel, n),
-        out_shape=(jax.ShapeDtypeStruct(queries.shape, BF16), landed, landed),
-        in_specs=[smem] * 4 + [anywhere] * 7,
-        out_specs=(vmem, vmem, vmem),
+        out_shape=(
+            jax.ShapeDtypeStruct((rows_sr, query_width), BF16),
+            jax.ShapeDtypeStruct((KVH, rows, HD), F32),
+            jax.ShapeDtypeStruct((rows, KVH), F32),
+            jax.ShapeDtypeStruct((rows, KVH), F32),
+            jax.ShapeDtypeStruct((2, most_pages + 1, page_rows, kv_width), BF16),
+            jax.ShapeDtypeStruct((rows_sr, extra), F32),
+        ),
+        in_specs=[smem] * 4 + [hbm] * 7,
+        out_specs=(hbm,) * 6,
         scratch_shapes=[
+            pltpu.VMEM((rows_sr, query_width), BF16),
+            pltpu.VMEM((KVH, rows, HD), F32),
+            pltpu.VMEM((rows, KVH), F32),
+            pltpu.VMEM((rows, KVH), F32),
+            pltpu.VMEM((2, most_pages + 1, page_rows, kv_width), BF16),
+            pltpu.VMEM((rows_sr, extra), F32),
             pltpu.VMEM(queries.shape, BF16),
             pltpu.VMEM((2,) + new_keys.shape, BF16),
             pltpu.VMEM(pool_keys.shape, BF16),
@@ -356,14 +456,10 @@
             pltpu.VMEM((2, n * most_pages, SUB, LANES), BF16),
             pltpu.VMEM((blocks * most_pages, page_rows, kv_width), BF16),
             pltpu.VMEM((blocks * most_pages, page_rows, kv_width), BF16),
-            pltpu.VMEM((2, most_pages + 1, page_rows, kv_width), BF16),
             pltpu.VMEM((rows_sr, query_width), F32),
-            pltpu.VMEM((rows_sr, query_width), F32),
-            pltpu.VMEM((KVH, rows, HD), F32),
-            pltpu.VMEM((KVH, rows, HD), F32),
-            pltpu.VMEM((KVH, rows, HD), F32),
             pltpu.SMEM(turn_lengths.shape, jnp.int32),
             pltpu.SMEM((n * most_pages,), jnp.int32),
+            pltpu.SemaphoreType.DMA((7,)),
             pltpu.SemaphoreType.DMA((7,)),
             pltpu.SemaphoreType.DMA((4,)),
             pltpu.SemaphoreType.DMA((2, spread)),
@@ -387,6 +483,25 @@
         turn_keys.reshape(paged),
         turn_values.reshape(paged),
     )
+    landed = jax.ShapeDtypeStruct((most_pages, page_rows, kv_width), BF16)
+    attended, landed_keys, landed_values = pl.pallas_call(
+        finish,
+        out_shape=(jax.ShapeDtypeStruct(queries.shape, BF16), landed, landed),
+        in_specs=[hbm] * 6,
+        out_specs=(vmem, hbm, hbm),
+        scratch_shapes=[
+            pltpu.VMEM((rows_sr, query_width), BF16),
+            pltpu.VMEM((KVH, rows, HD), F32),
+            pltpu.VMEM((rows, KVH), F32),
+            pltpu.VMEM((rows, KVH), F32),
+            pltpu.VMEM((2, most_pages + 1, page_rows, kv_width), BF16),
+            pltpu.VMEM((rows_sr, extra), F32),
+            pltpu.VMEM((rows_sr, query_width), F32),
+            pltpu.SemaphoreType.DMA((7,)),
+            pltpu.SemaphoreType.DMA((2,)),
+        ],
+        compiler_params=pltpu.CompilerParams(vmem_limit_bytes=60 * 1024 * 1024),
+    )(*parts)
     span = most_pages * page_rows
     return (
         attended,

time: 29.9 us -> 27.3 us (0.913)
  local copies, waits for them, and re-layouts: 4.93 us -> 0 us
  Pallas kernels: 24.1 us -> 26.4 us
    unnamed x3 -> x0, local copies, waits for them, and re-layouts: 4.93 us -> none
    pallas_call x0 -> x1, Pallas kernels: none -> 4.74 us  [per_device(): pl.pallas_call(finish, out_shape=(jax.ShapeDtypeStruct(queries.shape, BF1...]
    pallas_call x1, Pallas kernels: 24.1 us -> 21.7 us  [per_device(): pl.pallas_call(functools.partial(kernel, n), out_shape=(jax.ShapeDtypeStr...]
where the time goes in v2:
time: 27.3 us; the launch traced here: 27.1 us
  Pallas kernels  26.4 us (97%)
  between operations  0.64 us (2%)
    pallas_call x1, Pallas kernels, per_device(): pl.pallas_call(functools.partial(kernel, n), out_shape=(jax.ShapeDtypeStr...  21.7 us
    pallas_call x1, Pallas kernels, per_device(): pl.pallas_call(finish, out_shape=(jax.ShapeDtypeStruct(queries.shape, BF1...  4.74 us

profile of v2, /device:TPU:0, one launch (start us, length us, event | category | flops | bytes accessed | tf_op | source)
XLA Modules:
  0.0 27.1 jit_solution(6681989387504422293)
XLA Ops:
  0.6 21.7 %shard_map.130 = (bf16[16,8192]{1,0:T(8,128)(2,1)}, f32[8,128,128]{2,1,0:T(8,128)}, f32[128,8]{1,0:T(8,128)}, f32[128,8]{1,0:T(8,128)}, bf16[2,6,16,1024]{3,2,1,0:T(8,128)(2,1)}, /*index=5*/f32[16,96]{1,0:T(8,128)}) custom-call(s32[4,16]{1,0:T(4,128)} %table_ref.1, s32[4]{0:T(128)} %cached_ref.1, s32[16]{0:T(128)} %lengths_ref.1, s32[16]{0:T(128)} %slots_ref.1, ...), custom_call_target="tpu_custom_call" | custom-call | tf_op jit(solution)/shard_map/pallas_call | solution.py:430
  22.3 4.7 %shard_map.131 = (bf16[4,4,8192]{2,1,0:T(4,128)(2,1)}, bf16[5,16,1024]{2,1,0:T(8,128)(2,1)}, bf16[5,16,1024]{2,1,0:T(8,128)(2,1)}) custom-call(bf16[16,8192]{1,0:T(8,128)(2,1)} %get-tuple-element.12.qb_hbm, f32[8,128,128]{2,1,0:T(8,128)} %get-tuple-element.13.acc_hbm, f32[128,8]{1,0:T(8,128)} %get-tuple-element.14.mx_hbm, ...), custom_call_target="tpu_custom_call" | custom-call | tf_op jit(solution)/shard_map/pallas_call | solution.py:487
